TPU v7x, 8 devices: a whole 2x2x1 slice. The times are simulated.
8 devices in a mesh: vp: 8 (over z, y, x, core).
Axes of the slice: x: 2, y: 2, z: 1, core: 2. Of those that a mesh axis runs over, the one named last changes fastest.
Arguments:
- hidden: bfloat16 [32, 2048], replicated
- ln_weight: bfloat16 [2048], replicated
- ln_bias: bfloat16 [2048], replicated
- embedding: bfloat16 [250880, 2048], P('vp')
- temperature: float32 [], replicated
- cand_ids: int32 [32, 128], replicated
Outputs:
- output 1: float32 [32, 250880], P(None, 'vp')
- output 2: float32 [32, 128], replicated
All inputs are finite; a program needn't handle non-finite values.
Results may differ from a plain program's by a relative error of at most 0.001.
Values sent between devices are 32-bit elements.
A program may use at most 1 GiB of HBM per device.

v0:
```python
import jax
import jax.numpy as jnp
from jax import lax
from jax.sharding import PartitionSpec as P, NamedSharding


def layer_norm(hidden, ln_weight, ln_bias):
    hidden_f32 = hidden.astype(jnp.float32)
    row_mean = jnp.mean(hidden_f32, axis=-1, keepdims=True)
    centered = hidden_f32 - row_mean
    row_var = jnp.mean(centered * centered, axis=-1, keepdims=True)
    scaled = centered * lax.rsqrt(row_var + 1e-5)
    return (scaled * ln_weight.astype(jnp.float32) + ln_bias.astype(jnp.float32)).astype(jnp.bfloat16)


def solution(mesh):
    axis_name = mesh.axis_names[0]

    def per_device(hidden, ln_weight, ln_bias, emb_shard, value_a11, cand_ids):
        normed = layer_norm(hidden, ln_weight, ln_bias)
        shard_logits = lax.dot_general(normed, emb_shard, (((1,), (1,)), ((), ())), preferred_element_type=jnp.float32) / value_a11
        full_logits = lax.all_gather(shard_logits, axis_name, axis=1, tiled=True)
        row_max = jnp.max(full_logits, axis=1, keepdims=True)
        exp_sum = jnp.sum(jnp.exp(full_logits - row_max), axis=1, keepdims=True)
        log_norm = row_max + jnp.log(exp_sum)
        shard_lp = shard_logits - log_norm
        cand_lp = jnp.take_along_axis(full_logits, cand_ids, axis=1) - log_norm
        return shard_lp, cand_lp

    return jax.shard_map(
        per_device,
        mesh=mesh,
        in_specs=(P(), P(), P(), P(axis_name, None), P(), P()),
        out_specs=(P(None, axis_name), P()),
        check_vma=False,
    )
```

profile of v0, /device:TPU:0, one launch (start us, length us, event | category | flops | bytes accessed | tf_op | source)
XLA Modules:
  0.0 303.8 jit_solution(14864946977646517109)
XLA Ops:
  7.2 0.0 all-gather.2.cloned.1.call-start
  7.9 1.0 convert_reduce_fusion
  8.9 1.1 fusion.2
  10.0 0.7 convert_element_type.13
  10.7 0.7 convert_element_type.14
  11.4 49.3 %convolution_divide_fusion = f32[32,31360]{1,0:T(8,128)} fusion(bf16[31360,2048]{1,0:T(8,128)(2,1)} %param.9, f32[]{:T(128)S(6)} %copy.8, bf16[32,2048]{1,0:T(8,128)(2,1)} %param.6, f32[2048]{0:T(1024)S(1)} %convert_element_type.14, f32[2048]{0:T(1024)S(1)} %convert_element_type.13, f32[32]{0:T(128)S(1)} %add_rsqrt_fusion, f32[32]{0:T(128)S(1)} %broadcast_multiply_fusion), kind=kOutput, calls=%fused_computation.1 | convolution fusion | flops 4111814656 | bytes 132612352 | tf_op jit(solution)/shard_map/dot_general | solution.py:21
  60.8 0.0 copy-start.1
  60.8 0.0 all-gather.2.cloned.1.call-update
  60.8 0.7 copy-done.1
  61.5 151.4 %all-gather.2.cloned.1.call-done = f32[32,250880]{1,0:T(8,128)} async-done(((f32[32,31360]{1,0:T(8,128)}), f32[32,250880]{1,0:T(8,128)}) %all-gather.2.cloned.1.call-update) | async-done | bytes 32112656 | tf_op jit(solution)/shard_map/all_gather | solution.py:22
  212.9 14.6 %reduce_max.9 = f32[32]{0:T(128)S(1)} reduce(f32[32,250880]{1,0:T(8,128)} %all-gather.2.cloned.1.call-done, f32[]{:T(128)} %constant.21.clone.1), dimensions={1}, to_apply=%region_2.0 | reduce | flops 8028128 | bytes 32112772 | tf_op jit(solution)/shard_map/reduce_max | solution.py:23
  227.5 0.0 copy-start
  227.5 15.2 %exponential_reduce_fusion = f32[32]{0:T(128)S(1)} fusion(f32[32,250880]{1,0:T(8,128)} %all-gather.2.cloned.1.call-done, f32[32]{0:T(128)S(1)} %reduce_max.9), kind=kLoop, calls=%fused_computation.2 | loop fusion | flops 16056288 | bytes 32112896 | tf_op jit(solution)/shard_map/reduce_sum | solution.py:24
  242.7 0.0 copy-done
  242.7 2.3 broadcast_subtract_fusion
  245.0 51.2 %gather_fusion = f32[4096]{0:T(1024)S(1)} fusion(f32[32,250880]{1,0:T(8,128)} %all-gather.2.cloned.1.call-done, s32[4096]{0:T(1024)S(1)} %fusion.12), kind=kCustom, calls=%fused_computation | custom fusion | bytes 65536 | tf_op jit(solution)/shard_map/jit(take_along_axis)/gather | solution.py:27
  296.2 0.7 fusion.11
  (4 shorter events, 0.0 us)
Async XLA Ops:
  7.2 205.7 %all-gather.2.cloned.1.call-start = ((), (), s32[]{:S(2)}) async-start(), calls=%async_computation | async-start | bytes 36126720 | tf_op jit(solution)/shard_map/all_gather | solution.py:22
  60.8 0.7 copy-start.1
  227.5 15.2 %copy-start = (f32[32,31360]{1,0:T(8,128)S(1)}, f32[32,31360]{1,0:T(8,128)}, u32[]{:S(2)}) copy-start(f32[32,31360]{1,0:T(8,128)} %convolution_divide_fusion) | copy-start | bytes 12042244
Sparse Core Ops, SparseCore 0:
  60.9 151.9 all-gather.1
where the time goes:
time: 306 us; the launch traced here: 304 us
  waiting for transfers between devices  151 us (49%)
  local copies, waits for them, and re-layouts  51.9 us (17%)
  matrix products  49.3 us (16%)
  other arithmetic  36.3 us (12%)
  between operations  14.7 us (5%)
    all_gather x1, waiting for transfers between devices, per_device(): full_logits = lax.all_gather(shard_logits, axis_name, axis=1, tiled=True)  151 us
    gather x1, local copies, waits for them, and re-layouts, per_device(): cand_lp = jnp.take_along_axis(full_logits, cand_ids, axis=1) - log_norm  51.2 us
    dot_general x1, matrix products, per_device(): lax.dot_general(normed, emb_shard, (((1,), (1,)), ((), ())), preferred_el...  49.3 us
    reduce_sum x1, other arithmetic, per_device(): exp_sum = jnp.sum(jnp.exp(full_logits - row_max), axis=1, keepdims=True)  15.2 us
    reduce_max x1, other arithmetic, per_device(): row_max = jnp.max(full_logits, axis=1, keepdims=True)  14.6 us
  transfers between devices with their start and end apart: 1, of which 1 were waited for; matrix products, arithmetic and copies ran while one was open for 0% of the time, Pallas kernels for 0%

commit v1 on v0

v1 whole, which is shorter than its diff:
```python
import functools

import jax
import jax.numpy as jnp
from jax import lax
from jax.experimental import pallas as pl
from jax.experimental.pallas import tpu as pltpu
from jax.sharding import PartitionSpec as P

LANES = 128
TILE = 256
CHUNK = 2048
SLOTS = 4
PIECE = 4480
OFFSETS = [(1, 1, 0), (1, 1, 1), (1, 0, 0), (1, 0, 1), (0, 1, 0), (0, 1, 1), (0, 0, 1)]


def peers_of(me):
    y, x, core = me // 4, lax.rem(me // 2, 2), lax.rem(me, 2)
    return [lax.rem(y + dy, 2) * 4 + lax.rem(x + dx, 2) * 2 + lax.rem(core + dc, 2) for dy, dx, dc in OFFSETS]


def stream_kernel(axis, rows, x_ref, w_ref, b_ref, t_ref, cand_ref, emb_ref, z_ref, norm_ref, candz_ref,
                  ebuf, a_ref, m_ref, s_ref, q_ref, q_recv, st_send, st_recv,
                  ecopy_sem, q_send_sem, q_recv_sem, st_send_sem, st_recv_sem):
    me = lax.axis_index(axis)
    peers = peers_of(me)
    barrier = pltpu.get_barrier_semaphore()
    for peer in peers:
        pl.semaphore_signal(barrier, inc=1, device_id=(peer,), device_id_type=pl.DeviceIdType.MESH)

    full = rows // CHUNK
    tail = rows - full * CHUNK

    def fetch(i, slot, size=CHUNK):
        return pltpu.make_async_copy(
            emb_ref.at[pl.ds(i * CHUNK, size), :], ebuf.at[slot, pl.ds(0, size), :], ecopy_sem.at[slot])

    for i in range(SLOTS - 1):
        fetch(i, i).start()

    x = x_ref[...].astype(jnp.float32)
    centered = x - jnp.mean(x, axis=-1, keepdims=True)
    var = jnp.mean(centered * centered, axis=-1, keepdims=True)
    scaled = centered * lax.rsqrt(var + 1e-5)
    a_ref[...] = (scaled * w_ref[...].astype(jnp.float32) + b_ref[...].astype(jnp.float32)).astype(jnp.bfloat16)
    m_ref[...] = jnp.full(m_ref.shape, -jnp.inf, jnp.float32)
    s_ref[...] = jnp.zeros(s_ref.shape, jnp.float32)
    q_ref[...] = jnp.zeros(q_ref.shape, jnp.float32)
    temp = t_ref[0]

    def logits(i, slot, size=CHUNK):
        base = i * CHUNK
        for t in range(0, size, TILE):
            n = min(TILE, size - t)
            z = lax.dot_general(a_ref[...], ebuf[slot, t:t + n, :], (((1,), (1,)), ((), ())),
                                preferred_element_type=jnp.float32) / temp
            z_ref[:, pl.ds(pl.multiple_of(base + t, LANES), n)] = z

    def statistics(i, size=CHUNK):
        base = i * CHUNK
        cand = cand_ref[...] - me * rows - base
        lane, group = jnp.bitwise_and(cand, LANES - 1), jnp.right_shift(cand, 7)
        tiles = [z_ref[:, pl.ds(pl.multiple_of(base + t, LANES), LANES)] for t in range(0, size, LANES)]
        old = m_ref[...]
        new = functools.reduce(jnp.maximum, tiles, old)
        total = s_ref[...] * jnp.exp(old - new)
        q = q_ref[...]
        for k, z in enumerate(tiles):
            total = total + jnp.exp(z - new)
            q = jnp.where(group == k, jnp.take_along_axis(z, lane, axis=1, mode="promise_in_bounds"), q)
        m_ref[...] = new
        s_ref[...] = total
        q_ref[...] = q

    fetch(SLOTS - 1, SLOTS - 1).start()
    fetch(0, 0).wait()
    logits(0, 0)

    @pl.loop(1, full - SLOTS + 1)
    def _(i):
        fetch(i + SLOTS - 1, lax.rem(i + SLOTS - 1, SLOTS)).start()
        fetch(i, lax.rem(i, SLOTS)).wait()
        statistics(i - 1)
        logits(i, lax.rem(i, SLOTS))

    fetch(full, full % SLOTS, tail).start()

    @pl.loop(full - SLOTS + 1, full)
    def _(i):
        fetch(i, lax.rem(i, SLOTS)).wait()
        statistics(i - 1)
        logits(i, lax.rem(i, SLOTS))

    fetch(full, full % SLOTS, tail).wait()
    statistics(full - 1)
    logits(full, full % SLOTS, tail)
    statistics(full, tail)

    m = m_ref[...]
    row_max = jnp.max(m, axis=1, keepdims=True)
    row_sum = jnp.sum(s_ref[...] * jnp.exp(m - row_max), axis=1, keepdims=True)
    local = row_max + jnp.log(row_sum)
    diagonal = lax.broadcasted_iota(jnp.int32, m.shape, 0) == lax.broadcasted_iota(jnp.int32, m.shape, 1)
    packed = jnp.sum(jnp.where(diagonal, local, 0.0), axis=0, keepdims=True)
    st_send[...] = packed
    st_recv[me] = packed

    pl.semaphore_wait(barrier, len(peers))
    copies = []
    for k, peer in enumerate(peers):
        where = dict(device_id=(peer,), device_id_type=pl.DeviceIdType.MESH)
        copies.append((
            pltpu.make_async_remote_copy(src_ref=q_ref, dst_ref=q_recv.at[k], send_sem=q_send_sem.at[k],
                                         recv_sem=q_recv_sem.at[k], **where),
            pltpu.make_async_remote_copy(src_ref=st_send, dst_ref=st_recv.at[me], send_sem=st_send_sem.at[k],
                                         recv_sem=st_recv_sem.at[k], **where)))
    for q_copy, st_copy in copies:
        st_copy.start()
    for q_copy, st_copy in copies:
        q_copy.start()
    for q_copy, st_copy in copies:
        st_copy.wait()
    parts = [st_recv[p] for p in range(8)]
    top = functools.reduce(jnp.maximum, parts)
    norm = top + jnp.log(functools.reduce(jnp.add, [jnp.exp(p - top) for p in parts]))
    norm = jnp.sum(jnp.where(diagonal, norm, 0.0), axis=1, keepdims=True)
    norm_ref[...] = jnp.broadcast_to(norm, norm_ref.shape)
    q = q_ref[...]
    for k, (q_copy, st_copy) in enumerate(copies):
        q_copy.wait()
        q = q + q_recv[k]
    candz_ref[...] = q


def finish_kernel(z_ref, norm_ref, candz_ref, lp_ref, q_ref, buf, sem):
    norm = norm_ref[...]
    columns = z_ref.shape[1]
    copies = []
    for n, start in enumerate(range(0, columns, PIECE)):
        for c in range(start, start + PIECE, LANES):
            buf[:, c:c + LANES] = z_ref[:, c:c + LANES] - norm
        copies.append(pltpu.make_async_copy(buf.at[:, pl.ds(start, PIECE)], lp_ref.at[:, pl.ds(start, PIECE)], sem.at[n]))
        copies[-1].start()
    q_ref[...] = candz_ref[...] - norm
    for copy in copies:
        copy.wait()


def solution(mesh):
    axis = mesh.axis_names[0]

    def per_device(hidden, ln_weight, ln_bias, emb, temperature, cand_ids):
        batch, width = hidden.shape
        rows = emb.shape[0]
        vmem = pl.BlockSpec(memory_space=pltpu.VMEM)
        f32 = jnp.float32
        dma = pltpu.SemaphoreType.DMA
        z, norm, candz = pl.pallas_call(
            functools.partial(stream_kernel, axis, rows),
            out_shape=(pltpu.VMEM((batch, rows), f32), pltpu.VMEM((batch, LANES), f32),
                       pltpu.VMEM((batch, LANES), f32)),
            in_specs=[vmem, vmem, vmem, pl.BlockSpec(memory_space=pltpu.SMEM), vmem,
                      pl.BlockSpec(memory_space=pl.ANY)],
            out_specs=(vmem, vmem, vmem),
            scratch_shapes=[
                pltpu.VMEM((SLOTS, CHUNK, width), jnp.bfloat16),
                pltpu.VMEM((batch, width), jnp.bfloat16),
                pltpu.VMEM((batch, LANES), f32),
                pltpu.VMEM((batch, LANES), f32),
                pltpu.VMEM((batch, LANES), f32),
                pltpu.VMEM((7, batch, LANES), f32),
                pltpu.VMEM((1, LANES), f32),
                pltpu.VMEM((8, 1, LANES), f32),
                dma((SLOTS,)), dma((7,)), dma((7,)), dma((7,)), dma((7,)),
            ],
            compiler_params=pltpu.CompilerParams(
                collective_id=0, has_side_effects=True, vmem_limit_bytes=44 * 1024 * 1024),
        )(hidden, ln_weight.reshape(1, width), ln_bias.reshape(1, width), temperature.reshape(1), cand_ids, emb)
        return pl.pallas_call(
            finish_kernel,
            out_shape=(jax.ShapeDtypeStruct((batch, rows), f32), jax.ShapeDtypeStruct((batch, LANES), f32)),
            in_specs=[vmem, vmem, vmem],
            out_specs=(pl.BlockSpec(memory_space=pl.ANY), vmem),
            scratch_shapes=[pltpu.VMEM((batch, rows), f32), dma((rows // PIECE,))],
            compiler_params=pltpu.CompilerParams(vmem_limit_bytes=16 * 1024 * 1024),
        )(z, norm, candz)

    return jax.shard_map(
        per_device,
        mesh=mesh,
        in_specs=(P(), P(), P(), P(axis, None), P(), P()),
        out_specs=(P(None, axis), P()),
        check_vma=False,
    )
```

time: 306 us -> 56.9 us (0.19)
  waiting for transfers between devices: 151 us -> 0 us
  Pallas kernels: 0 us -> 52.4 us
  matrix products: 49.3 us -> 0 us
  local copies, waits for them, and re-layouts: 51.9 us -> 3.01 us
  other arithmetic: 36.3 us -> 0 us
  between operations: 14.7 us -> 1.29 us
    all_gather x1 -> x0, waiting for transfers between devices: 151 us -> none  [per_device(): full_logits = lax.all_gather(shard_logits, axis_name, axis=1, tiled=True)]
    pallas_call x0 -> x2, Pallas kernels: none -> 52.4 us  [the longest x1 49.7 us: per_device(): pl.pallas_call(functools.partial(stream_kernel, axis, rows), out_shape=(p...]
    gather x1 -> x0, local copies, waits for them, and re-layouts: 51.2 us -> none  [per_device(): cand_lp = jnp.take_along_axis(full_logits, cand_ids, axis=1) - log_norm]
    dot_general x1 -> x0, matrix products: 49.3 us -> none  [per_device(): lax.dot_general(normed, emb_shard, (((1,), (1,)), ((), ())), preferred_el...]
    reduce_sum x3 -> x0, other arithmetic: 17.3 us -> none  [the longest x1 15.2 us: per_device(): exp_sum = jnp.sum(jnp.exp(full_logits - row_max), axis=1, keepdims=True)]
    reduce_max x1 -> x0, other arithmetic: 14.6 us -> none  [per_device(): row_max = jnp.max(full_logits, axis=1, keepdims=True)]
  transfers between devices with their start and end apart: 1 -> 0, of which waited for: 1 -> 0; matrix products, arithmetic and copies ran while one was open for 0% -> 0% of each run, Pallas kernels for 0% -> 0%
where the time goes in v1:
time: 56.9 us; the launch traced here: 56.7 us
  Pallas kernels  52.4 us (92%)
  local copies, waits for them, and re-layouts  3.01 us (5%)
  between operations  1.29 us (2%)
    pallas_call x1, Pallas kernels, per_device(): pl.pallas_call(functools.partial(stream_kernel, axis, rows), out_shape=(p...  49.7 us
    pallas_call x1, Pallas kernels, per_device(): pl.pallas_call(finish_kernel, out_shape=(jax.ShapeDtypeStruct((batch, row...  2.65 us
    unnamed x4, local copies, waits for them, and re-layouts  1.62 us

profile of v1, /device:TPU:0, one launch (start us, length us, event | category | flops | bytes accessed | tf_op | source)
XLA Modules:
  0.0 56.7 jit_solution(14034261672715992880)
XLA Ops:
  1.3 0.7 %reshape.13.w_ref = bf16[1,2048]{1,0:T(2,128)(2,1)S(1)} reshape(bf16[2048]{0:T(1024)(128)(2,1)} %param.7) | data formatting | bytes 8192 | tf_op jit(solution)/shard_map/reshape | solution.py:179
  2.0 0.7 %reshape.14.b_ref = bf16[1,2048]{1,0:T(2,128)(2,1)S(1)} reshape(bf16[2048]{0:T(1024)(128)(2,1)} %param.8) | data formatting | bytes 8192 | tf_op jit(solution)/shard_map/reshape | solution.py:179
  2.7 0.0 copy-start
  2.7 0.9 %copy-done = bf16[32,2048]{1,0:T(8,128)(2,1)S(1)} copy-done((bf16[32,2048]{1,0:T(8,128)(2,1)S(1)}, bf16[32,2048]{1,0:T(8,128)(2,1)}, u32[]{:S(2)}) %copy-start) | copy-done | bytes 131096
  3.6 0.0 copy-start.1
  3.6 0.7 %copy-done.1 = s32[32,128]{1,0:T(8,128)S(1)} copy-done((s32[32,128]{1,0:T(8,128)S(1)}, s32[32,128]{1,0:T(8,128)}, u32[]{:S(2)}) %copy-start.1) | copy-done | bytes 16408
  4.3 49.7 %shard_map.77 = (f32[32,31360]{1,0:T(8,128)S(1)}, f32[32,128]{1,0:T(8,128)S(1)}, f32[32,128]{1,0:T(8,128)S(1)}) custom-call(bf16[32,2048]{1,0:T(8,128)(2,1)S(1)} %copy-done, bf16[1,2048]{1,0:T(2,128)(2,1)S(1)} %reshape.13.w_ref, bf16[1,2048]{1,0:T(2,128)(2,1)S(1)} %reshape.14.b_ref, f32[1]{0:T(128)} %bitcast.1.t_ref, s32[32,128]{1,0:T(8,128)S(1)} %copy-done.1, ...), custom_call_target="tpu_custom_call" | custom-call | tf_op jit(solution)/shard_map/pallas_call | solution.py:159
  54.0 2.6 %shard_map.78 = (f32[32,31360]{1,0:T(8,128)}, f32[32,128]{1,0:T(8,128)}) custom-call(f32[32,31360]{1,0:T(8,128)S(1)} %get-tuple-element.5.z_ref, f32[32,128]{1,0:T(8,128)S(1)} %get-tuple-element.6.norm_ref, f32[32,128]{1,0:T(8,128)S(1)} %get-tuple-element.7.candz_ref), custom_call_target="tpu_custom_call" | custom-call | tf_op jit(solution)/shard_map/pallas_call | solution.py:180
Async XLA Ops:
  2.7 0.9 %copy-start = (bf16[32,2048]{1,0:T(8,128)(2,1)S(1)}, bf16[32,2048]{1,0:T(8,128)(2,1)}, u32[]{:S(2)}) copy-start(bf16[32,2048]{1,0:T(8,128)(2,1)} %x_ref.1) | copy-start | bytes 393220
  3.6 0.7 %copy-start.1 = (s32[32,128]{1,0:T(8,128)S(1)}, s32[32,128]{1,0:T(8,128)}, u32[]{:S(2)}) copy-start(s32[32,128]{1,0:T(8,128)} %cand_ref.1) | copy-start | bytes 49156

commit v2 on v1

v2 whole, which is shorter than its diff:
```python
import functools

import jax
import jax.numpy as jnp
from jax import lax
from jax.experimental import pallas as pl
from jax.experimental.pallas import tpu as pltpu
from jax.sharding import PartitionSpec as P

LANES = 128
CHUNK = 896
SLOTS = 8
DOTS = ((0, 256, False), (256, 256, True), (512, 128, False), (640, 256, True))
PIECES = (896, 1792, 3584, 6272, 6272, 6272, 6272)
OFFSETS = [(1, 1, 0), (1, 1, 1), (1, 0, 0), (1, 0, 1), (0, 1, 0), (0, 1, 1), (0, 0, 1)]
MESH = pl.DeviceIdType.MESH


def peers_of(me):
    y, x, core = me // 4, lax.rem(me // 2, 2), lax.rem(me, 2)
    return [lax.rem(y + dy, 2) * 4 + lax.rem(x + dx, 2) * 2 + lax.rem(core + dc, 2) for dy, dx, dc in OFFSETS]


def stream_kernel(axis, rows, t_ref, x_hbm, w_hbm, b_hbm, cand_hbm, emb_hbm, z_ref, norm_ref, candz_ref,
                  ebuf, et_ref, x_ref, w_ref, b_ref, cand_ref, a_ref, m_ref, s_ref, msg_ref, recv_ref,
                  ecopy_sem, in_sem, send_sem, recv_sem):
    batch, width = x_ref.shape
    chunks = rows // CHUNK
    inputs = [pltpu.make_async_copy(src, dst, in_sem.at[n]) for n, (src, dst) in enumerate(
        [(x_hbm, x_ref), (w_hbm, w_ref), (b_hbm, b_ref), (cand_hbm, cand_ref)])]
    for copy in inputs:
        copy.start()

    def fetch(i, slot):
        return pltpu.make_async_copy(emb_hbm.at[pl.ds(i * CHUNK, CHUNK), :], ebuf.at[slot], ecopy_sem.at[slot])

    for i in range(SLOTS):
        fetch(i, i).start()

    me = lax.axis_index(axis)
    peers = peers_of(me)
    barrier = pltpu.get_barrier_semaphore()
    for peer in peers:
        pl.semaphore_signal(barrier, inc=1, device_id=(peer,), device_id_type=MESH)

    for copy in inputs:
        copy.wait()
    x = x_ref[...].astype(jnp.float32)
    centered = x - jnp.mean(x, axis=-1, keepdims=True)
    var = jnp.mean(centered * centered, axis=-1, keepdims=True)
    scaled = centered * lax.rsqrt(var + 1e-5)
    gain, bias = w_ref[...].astype(jnp.float32), b_ref[...].astype(jnp.float32)
    for k in range(width // LANES):
        part = scaled[:, k * LANES:(k + 1) * LANES] * gain[k:k + 1, :] + bias[k:k + 1, :]
        a_ref[:, k * LANES:(k + 1) * LANES] = part.astype(jnp.bfloat16)
    m_ref[...] = jnp.full(m_ref.shape, -jnp.inf, jnp.float32)
    s_ref[...] = jnp.zeros(s_ref.shape, jnp.float32)
    msg_ref[...] = jnp.zeros(msg_ref.shape, jnp.float32)
    temp = t_ref[0]

    def logits(i, slot):
        for n, (first, size, flip) in enumerate(DOTS):
            tile = ebuf[slot, first:first + size, :]
            if flip:
                et_ref[n, :, :size] = tile.T
                z = jnp.dot(a_ref[...], et_ref[n, :, :size], preferred_element_type=jnp.float32)
            else:
                z = lax.dot_general(tile, a_ref[...], (((1,), (1,)), ((), ())), preferred_element_type=jnp.float32).T
            z_ref[:, pl.ds(pl.multiple_of(i * CHUNK + first, LANES), size)] = z / temp

    def statistics(i):
        cand = cand_ref[...] - me * rows - i * CHUNK
        lane, group = jnp.bitwise_and(cand, LANES - 1), jnp.right_shift(cand, 7)
        tiles = [z_ref[:, pl.ds(pl.multiple_of(i * CHUNK + t, LANES), LANES)] for t in range(0, CHUNK, LANES)]
        old = m_ref[...]
        new = functools.reduce(jnp.maximum, tiles, old)
        total = s_ref[...] * jnp.exp(old - new)
        q = msg_ref[:batch, :]
        for k, z in enumerate(tiles):
            total = total + jnp.exp(z - new)
            q = jnp.where(group == k, jnp.take_along_axis(z, lane, axis=1, mode="promise_in_bounds"), q)
        m_ref[...] = new
        s_ref[...] = total
        msg_ref[:batch, :] = q

    fetch(0, 0).wait()
    logits(0, 0)

    @pl.loop(1, chunks)
    def _(i):
        @pl.when(i + SLOTS - 1 < chunks)
        def _():
            fetch(i + SLOTS - 1, lax.rem(i + SLOTS - 1, SLOTS)).start()

        fetch(i, lax.rem(i, SLOTS)).wait()
        statistics(i - 1)
        logits(i, lax.rem(i, SLOTS))

    statistics(chunks - 1)
    m = m_ref[...]
    row_max = jnp.max(m, axis=1, keepdims=True)
    local = row_max + jnp.log(jnp.sum(s_ref[...] * jnp.exp(m - row_max), axis=1, keepdims=True))
    diagonal = lax.broadcasted_iota(jnp.int32, m.shape, 0) == lax.broadcasted_iota(jnp.int32, m.shape, 1)
    mine = jnp.sum(jnp.where(diagonal, local, 0.0), axis=0, keepdims=True)
    msg_ref[batch:batch + 1, :] = mine

    pl.semaphore_wait(barrier, len(peers))
    copies = [pltpu.make_async_remote_copy(
        src_ref=msg_ref, dst_ref=recv_ref.at[k], send_sem=send_sem.at[k], recv_sem=recv_sem.at[k],
        device_id=(peer,), device_id_type=MESH) for k, peer in enumerate(peers)]
    for copy in copies:
        copy.start()
    for copy in copies:
        copy.wait()
    parts = [mine] + [recv_ref[k, batch:batch + 1, :] for k in range(len(peers))]
    top = functools.reduce(jnp.maximum, parts)
    norm = top + jnp.log(functools.reduce(jnp.add, [jnp.exp(p - top) for p in parts]))
    norm = jnp.sum(jnp.where(diagonal, norm, 0.0), axis=1, keepdims=True)
    norm_ref[...] = jnp.broadcast_to(norm, norm_ref.shape)
    candz_ref[...] = functools.reduce(jnp.add, [recv_ref[k, :batch, :] for k in range(len(peers))], msg_ref[:batch, :])


def finish_kernel(z_ref, norm_ref, candz_ref, lp_hbm, q_ref, buf, sem):
    norm = norm_ref[...]
    copies, start = [], 0
    for n, size in enumerate(PIECES):
        for c in range(start, start + size, LANES):
            buf[:, c:c + LANES] = z_ref[:, c:c + LANES] - norm
        copies.append(pltpu.make_async_copy(buf.at[:, pl.ds(start, size)], lp_hbm.at[:, pl.ds(start, size)], sem.at[n]))
        copies[-1].start()
        start += size
    q_ref[...] = candz_ref[...] - norm
    for copy in copies:
        copy.wait()


def solution(mesh):
    axis = mesh.axis_names[0]

    def per_device(hidden, ln_weight, ln_bias, emb, temperature, cand_ids):
        batch, width = hidden.shape
        rows = emb.shape[0]
        vmem = pl.BlockSpec(memory_space=pltpu.VMEM)
        hbm = pl.BlockSpec(memory_space=pl.ANY)
        f32, bf16 = jnp.float32, jnp.bfloat16
        dma = pltpu.SemaphoreType.DMA
        block = (width // LANES, LANES)
        small = [hidden, ln_weight.reshape(block), ln_bias.reshape(block), cand_ids]
        small = [pltpu.with_memory_space_constraint(v, pltpu.HBM) for v in small]
        z, norm, candz = pl.pallas_call(
            functools.partial(stream_kernel, axis, rows),
            out_shape=(pltpu.VMEM((batch, rows), f32), pltpu.VMEM((batch, LANES), f32),
                       pltpu.VMEM((batch, LANES), f32)),
            in_specs=[pl.BlockSpec(memory_space=pltpu.SMEM)] + [hbm] * 5,
            out_specs=(vmem, vmem, vmem),
            scratch_shapes=[
                pltpu.VMEM((SLOTS, CHUNK, width), bf16),
                pltpu.VMEM((len(DOTS), width, 256), bf16),
                pltpu.VMEM((batch, width), bf16),
                pltpu.VMEM(block, bf16),
                pltpu.VMEM(block, bf16),
                pltpu.VMEM((batch, LANES), jnp.int32),
                pltpu.VMEM((batch, width), bf16),
                pltpu.VMEM((batch, LANES), f32),
                pltpu.VMEM((batch, LANES), f32),
                pltpu.VMEM((batch + 8, LANES), f32),
                pltpu.VMEM((len(OFFSETS), batch + 8, LANES), f32),
                dma((SLOTS,)), dma((4,)), dma((7,)), dma((7,)),
            ],
            compiler_params=pltpu.CompilerParams(
                collective_id=0, has_side_effects=True, vmem_limit_bytes=48 * 1024 * 1024),
        )(temperature.reshape(1), *small, emb)
        return pl.pallas_call(
            finish_kernel,
            out_shape=(jax.ShapeDtypeStruct((batch, rows), f32), jax.ShapeDtypeStruct((batch, LANES), f32)),
            in_specs=[vmem, vmem, vmem],
            out_specs=(hbm, vmem),
            scratch_shapes=[pltpu.VMEM((batch, rows), f32), dma((len(PIECES),))],
            compiler_params=pltpu.CompilerParams(vmem_limit_bytes=16 * 1024 * 1024),
        )(z, norm, candz)

    return jax.shard_map(
        per_device,
        mesh=mesh,
        in_specs=(P(), P(), P(), P(axis, None), P(), P()),
        out_specs=(P(None, axis), P()),
        check_vma=False,
    )
```

time: 56.9 us -> 50.5 us (0.89)
  Pallas kernels: 52.4 us -> 49.1 us
  local copies, waits for them, and re-layouts: 3.01 us -> 0 us
    pallas_call x1, Pallas kernels: 49.7 us -> 46.5 us  [per_device(): pl.pallas_call(functools.partial(stream_kernel, axis, rows), out_shape=(p...]
    unnamed x4 -> x0, local copies, waits for them, and re-layouts: 1.62 us -> none
    reshape x2 -> x0, local copies, waits for them, and re-layouts: 1.39 us -> none  [the longest x1 0.69 us: per_device(): ln_weight.reshape(1, width)]
where the time goes in v2:
time: 50.5 us; the launch traced here: 50.4 us
  Pallas kernels  49.1 us (97%)
  between operations  1.29 us (3%)
    pallas_call x1, Pallas kernels, per_device(): pl.pallas_call(functools.partial(stream_kernel, axis, rows), out_shape=(p...  46.5 us
    pallas_call x1, Pallas kernels, per_device(): pl.pallas_call(finish_kernel, out_shape=(jax.ShapeDtypeStruct((batch, row...  2.62 us

profile of v2, /device:TPU:0, one launch (start us, length us, event | category | flops | bytes accessed | tf_op | source)
XLA Modules:
  0.0 50.4 jit_solution(6871262277049122880)
XLA Ops:
  1.3 46.5 %shard_map.77 = (f32[32,31360]{1,0:T(8,128)S(1)}, f32[32,128]{1,0:T(8,128)S(1)}, f32[32,128]{1,0:T(8,128)S(1)}) custom-call(f32[1]{0:T(128)} %bitcast.3.t_ref, bf16[32,2048]{1,0:T(8,128)(2,1)} %x_hbm.1, bf16[16,128]{1,0:T(8,128)(2,1)} %bitcast.4, bf16[16,128]{1,0:T(8,128)(2,1)} %bitcast.5, s32[32,128]{1,0:T(8,128)} %cand_hbm.1, bf16[31360,2048]{1,0:T(8,128)(2,1)} %emb_hbm.1), custom_call_target="tpu_custom_call" | custom-call | tf_op jit(solution)/shard_map/pallas_call | solution.py:150
  47.7 2.6 %shard_map.78 = (f32[32,31360]{1,0:T(8,128)}, f32[32,128]{1,0:T(8,128)}) custom-call(f32[32,31360]{1,0:T(8,128)S(1)} %get-tuple-element.5.z_ref, f32[32,128]{1,0:T(8,128)S(1)} %get-tuple-element.6.norm_ref, f32[32,128]{1,0:T(8,128)S(1)} %get-tuple-element.7.candz_ref), custom_call_target="tpu_custom_call" | custom-call | tf_op jit(solution)/shard_map/pallas_call | solution.py:173

commit v3 on v2

--- a/solution.py
+++ b/solution.py
@@ -9,8 +9,8 @@
 
 LANES = 128
 CHUNK = 896
-SLOTS = 8
-DOTS = ((0, 256, False), (256, 256, True), (512, 128, False), (640, 256, True))
+SLOTS = 5
+DOTS = ((0, 128, False), (128, 256, False), (384, 256, True), (640, 256, True))
 PIECES = (896, 1792, 3584, 6272, 6272, 6272, 6272)
 OFFSETS = [(1, 1, 0), (1, 1, 1), (1, 0, 0), (1, 0, 1), (0, 1, 0), (0, 1, 1), (0, 0, 1)]
 MESH = pl.DeviceIdType.MESH
@@ -22,9 +22,9 @@
 
 
 def stream_kernel(axis, rows, t_ref, x_hbm, w_hbm, b_hbm, cand_hbm, emb_hbm, z_ref, norm_ref, candz_ref,
-                  ebuf, et_ref, x_ref, w_ref, b_ref, cand_ref, a_ref, m_ref, s_ref, msg_ref, recv_ref,
-                  ecopy_sem, in_sem, send_sem, recv_sem):
-    batch, width = x_ref.shape
+                  ebuf, et_ref, x_ref, w_ref, b_ref, cand_ref, a_ref, m_ref, s_ref, q_ref, q_recv, st_ref, st_recv,
+                  ecopy_sem, in_sem, q_sem, st_sem):
+    width = x_ref.shape[1]
     chunks = rows // CHUNK
     inputs = [pltpu.make_async_copy(src, dst, in_sem.at[n]) for n, (src, dst) in enumerate(
         [(x_hbm, x_ref), (w_hbm, w_ref), (b_hbm, b_ref), (cand_hbm, cand_ref)])]
@@ -55,7 +55,7 @@
         a_ref[:, k * LANES:(k + 1) * LANES] = part.astype(jnp.bfloat16)
     m_ref[...] = jnp.full(m_ref.shape, -jnp.inf, jnp.float32)
     s_ref[...] = jnp.zeros(s_ref.shape, jnp.float32)
-    msg_ref[...] = jnp.zeros(msg_ref.shape, jnp.float32)
+    q_ref[...] = jnp.zeros(q_ref.shape, jnp.float32)
     temp = t_ref[0]
 
     def logits(i, slot):
@@ -68,20 +68,26 @@
                 z = lax.dot_general(tile, a_ref[...], (((1,), (1,)), ((), ())), preferred_element_type=jnp.float32).T
             z_ref[:, pl.ds(pl.multiple_of(i * CHUNK + first, LANES), size)] = z / temp
 
-    def statistics(i):
+    def tiles_of(i):
+        return [z_ref[:, pl.ds(pl.multiple_of(i * CHUNK + t, LANES), LANES)] for t in range(0, CHUNK, LANES)]
+
+    def candidates(i):
         cand = cand_ref[...] - me * rows - i * CHUNK
         lane, group = jnp.bitwise_and(cand, LANES - 1), jnp.right_shift(cand, 7)
-        tiles = [z_ref[:, pl.ds(pl.multiple_of(i * CHUNK + t, LANES), LANES)] for t in range(0, CHUNK, LANES)]
+        q = q_ref[...]
+        for k, z in enumerate(tiles_of(i)):
+            q = jnp.where(group == k, jnp.take_along_axis(z, lane, axis=1, mode="promise_in_bounds"), q)
+        q_ref[...] = q
+
+    def statistics(i):
+        tiles = tiles_of(i)
         old = m_ref[...]
         new = functools.reduce(jnp.maximum, tiles, old)
         total = s_ref[...] * jnp.exp(old - new)
-        q = msg_ref[:batch, :]
-        for k, z in enumerate(tiles):
+        for z in tiles:
             total = total + jnp.exp(z - new)
-            q = jnp.where(group == k, jnp.take_along_axis(z, lane, axis=1, mode="promise_in_bounds"), q)
         m_ref[...] = new
         s_ref[...] = total
-        msg_ref[:batch, :] = q
 
     fetch(0, 0).wait()
     logits(0, 0)
@@ -94,42 +100,54 @@
 
         fetch(i, lax.rem(i, SLOTS)).wait()
         statistics(i - 1)
+        candidates(i - 1)
         logits(i, lax.rem(i, SLOTS))
 
+    candidates(chunks - 1)
+    pl.semaphore_wait(barrier, len(peers))
+
+    def sends(src, dst, sems):
+        return [pltpu.make_async_remote_copy(
+            src_ref=src, dst_ref=dst.at[k], send_sem=sems.at[0, k], recv_sem=sems.at[1, k],
+            device_id=(peer,), device_id_type=MESH) for k, peer in enumerate(peers)]
+
+    q_copies = sends(q_ref, q_recv, q_sem)
+    for copy in q_copies:
+        copy.start()
     statistics(chunks - 1)
     m = m_ref[...]
     row_max = jnp.max(m, axis=1, keepdims=True)
     local = row_max + jnp.log(jnp.sum(s_ref[...] * jnp.exp(m - row_max), axis=1, keepdims=True))
     diagonal = lax.broadcasted_iota(jnp.int32, m.shape, 0) == lax.broadcasted_iota(jnp.int32, m.shape, 1)
     mine = jnp.sum(jnp.where(diagonal, local, 0.0), axis=0, keepdims=True)
-    msg_ref[batch:batch + 1, :] = mine
-
-    pl.semaphore_wait(barrier, len(peers))
-    copies = [pltpu.make_async_remote_copy(
-        src_ref=msg_ref, dst_ref=recv_ref.at[k], send_sem=send_sem.at[k], recv_sem=recv_sem.at[k],
-        device_id=(peer,), device_id_type=MESH) for k, peer in enumerate(peers)]
-    for copy in copies:
+    st_ref[...] = mine
+    st_copies = sends(st_ref, st_recv, st_sem)
+    for copy in st_copies:
         copy.start()
-    for copy in copies:
-        copy.wait()
-    parts = [mine] + [recv_ref[k, batch:batch + 1, :] for k in range(len(peers))]
+    for copy in st_copies:
+        copy.wait()
+    parts = [mine] + [st_recv[k] for k in range(len(peers))]
     top = functools.reduce(jnp.maximum, parts)
     norm = top + jnp.log(functools.reduce(jnp.add, [jnp.exp(p - top) for p in parts]))
     norm = jnp.sum(jnp.where(diagonal, norm, 0.0), axis=1, keepdims=True)
     norm_ref[...] = jnp.broadcast_to(norm, norm_ref.shape)
-    candz_ref[...] = functools.reduce(jnp.add, [recv_ref[k, :batch, :] for k in range(len(peers))], msg_ref[:batch, :])
-
-
-def finish_kernel(z_ref, norm_ref, candz_ref, lp_hbm, q_ref, buf, sem):
+    for copy in q_copies:
+        copy.wait()
+    candz_ref[...] = functools.reduce(jnp.add, [q_recv[k] for k in range(len(peers))], q_ref[...])
+
+
+def finish_kernel(z_ref, norm_ref, candz_ref, lp_hbm, q_hbm, buf, q_ref, sem):
     norm = norm_ref[...]
-    copies, start = [], 0
+    q_ref[...] = candz_ref[...] - norm
+    copies, start = [pltpu.make_async_copy(q_ref, q_hbm, sem.at[len(PIECES)])], 0
     for n, size in enumerate(PIECES):
         for c in range(start, start + size, LANES):
             buf[:, c:c + LANES] = z_ref[:, c:c + LANES] - norm
         copies.append(pltpu.make_async_copy(buf.at[:, pl.ds(start, size)], lp_hbm.at[:, pl.ds(start, size)], sem.at[n]))
         copies[-1].start()
         start += size
-    q_ref[...] = candz_ref[...] - norm
+        if n == 0:
+            copies[0].start()
     for copy in copies:
         copy.wait()
 
@@ -163,9 +181,11 @@
                 pltpu.VMEM((batch, width), bf16),
                 pltpu.VMEM((batch, LANES), f32),
                 pltpu.VMEM((batch, LANES), f32),
-                pltpu.VMEM((batch + 8, LANES), f32),
-                pltpu.VMEM((len(OFFSETS), batch + 8, LANES), f32),
-                dma((SLOTS,)), dma((4,)), dma((7,)), dma((7,)),
+                pltpu.VMEM((batch, LANES), f32),
+                pltpu.VMEM((len(OFFSETS), batch, LANES), f32),
+                pltpu.VMEM((1, LANES), f32),
+                pltpu.VMEM((len(OFFSETS), 1, LANES), f32),
+                dma((SLOTS,)), dma((4,)), dma((2, 7)), dma((2, 7)),
             ],
             compiler_params=pltpu.CompilerParams(
                 collective_id=0, has_side_effects=True, vmem_limit_bytes=48 * 1024 * 1024),
@@ -174,8 +194,9 @@
             finish_kernel,
             out_shape=(jax.ShapeDtypeStruct((batch, rows), f32), jax.ShapeDtypeStruct((batch, LANES), f32)),
             in_specs=[vmem, vmem, vmem],
-            out_specs=(hbm, vmem),
-            scratch_shapes=[pltpu.VMEM((batch, rows), f32), dma((len(PIECES),))],
+            out_specs=(hbm, hbm),
+            scratch_shapes=[pltpu.VMEM((batch, rows), f32), pltpu.VMEM((batch, LANES), f32),
+                            dma((len(PIECES) + 1,))],
             compiler_params=pltpu.CompilerParams(vmem_limit_bytes=16 * 1024 * 1024),
         )(z, norm, candz)
 

time: 50.5 us -> 50.3 us (level)
    pallas_call x1, Pallas kernels: 2.62 us -> 2.03 us  [per_device(): pl.pallas_call(finish_kernel, out_shape=(jax.ShapeDtypeStruct((batch, row...]
where the time goes in v3:
time: 50.3 us; the launch traced here: 50.2 us
  Pallas kernels  48.9 us (97%)
  between operations  1.29 us (3%)
    pallas_call x1, Pallas kernels, per_device(): pl.pallas_call(functools.partial(stream_kernel, axis, rows), out_shape=(p...  46.8 us
    pallas_call x1, Pallas kernels, per_device(): pl.pallas_call(finish_kernel, out_shape=(jax.ShapeDtypeStruct((batch, row...  2.03 us

profile of v3, /device:TPU:0, one launch (start us, length us, event | category | flops | bytes accessed | tf_op | source)
XLA Modules:
  0.0 50.2 jit_solution(9605097894051365294)
XLA Ops:
  1.3 46.8 %shard_map.77 = (f32[32,31360]{1,0:T(8,128)S(1)}, f32[32,128]{1,0:T(8,128)S(1)}, f32[32,128]{1,0:T(8,128)S(1)}) custom-call(f32[1]{0:T(128)} %bitcast.3.t_ref, bf16[32,2048]{1,0:T(8,128)(2,1)} %x_hbm.1, bf16[16,128]{1,0:T(8,128)(2,1)} %bitcast.4, bf16[16,128]{1,0:T(8,128)(2,1)} %bitcast.5, s32[32,128]{1,0:T(8,128)} %cand_hbm.1, bf16[31360,2048]{1,0:T(8,128)(2,1)} %emb_hbm.1), custom_call_target="tpu_custom_call" | custom-call | tf_op jit(solution)/shard_map/pallas_call | solution.py:168
  48.1 2.0 %shard_map.78 = (f32[32,31360]{1,0:T(8,128)}, f32[32,128]{1,0:T(8,128)}) custom-call(f32[32,31360]{1,0:T(8,128)S(1)} %get-tuple-element.5.z_ref, f32[32,128]{1,0:T(8,128)S(1)} %get-tuple-element.6.norm_ref, f32[32,128]{1,0:T(8,128)S(1)} %get-tuple-element.7.candz_ref), custom_call_target="tpu_custom_call" | custom-call | tf_op jit(solution)/shard_map/pallas_call | solution.py:193

commit v4 on v3

--- a/solution.py
+++ b/solution.py
@@ -12,13 +12,12 @@
 SLOTS = 5
 DOTS = ((0, 128, False), (128, 256, False), (384, 256, True), (640, 256, True))
 PIECES = (896, 1792, 3584, 6272, 6272, 6272, 6272)
-OFFSETS = [(1, 1, 0), (1, 1, 1), (1, 0, 0), (1, 0, 1), (0, 1, 0), (0, 1, 1), (0, 0, 1)]
+DEVICES = 8
 MESH = pl.DeviceIdType.MESH
 
 
 def peers_of(me):
-    y, x, core = me // 4, lax.rem(me // 2, 2), lax.rem(me, 2)
-    return [lax.rem(y + dy, 2) * 4 + lax.rem(x + dx, 2) * 2 + lax.rem(core + dc, 2) for dy, dx, dc in OFFSETS]
+    return [k + (k + DEVICES - me) // DEVICES for k in range(DEVICES - 1)]
 
 
 def stream_kernel(axis, rows, t_ref, x_hbm, w_hbm, b_hbm, cand_hbm, emb_hbm, z_ref, norm_ref, candz_ref,
@@ -104,16 +103,6 @@
         logits(i, lax.rem(i, SLOTS))
 
     candidates(chunks - 1)
-    pl.semaphore_wait(barrier, len(peers))
-
-    def sends(src, dst, sems):
-        return [pltpu.make_async_remote_copy(
-            src_ref=src, dst_ref=dst.at[k], send_sem=sems.at[0, k], recv_sem=sems.at[1, k],
-            device_id=(peer,), device_id_type=MESH) for k, peer in enumerate(peers)]
-
-    q_copies = sends(q_ref, q_recv, q_sem)
-    for copy in q_copies:
-        copy.start()
     statistics(chunks - 1)
     m = m_ref[...]
     row_max = jnp.max(m, axis=1, keepdims=True)
@@ -121,19 +110,38 @@
     diagonal = lax.broadcasted_iota(jnp.int32, m.shape, 0) == lax.broadcasted_iota(jnp.int32, m.shape, 1)
     mine = jnp.sum(jnp.where(diagonal, local, 0.0), axis=0, keepdims=True)
     st_ref[...] = mine
-    st_copies = sends(st_ref, st_recv, st_sem)
-    for copy in st_copies:
-        copy.start()
-    for copy in st_copies:
-        copy.wait()
+
+    pl.semaphore_wait(barrier, len(peers))
+
+    def send(src, dst, sems, peer):
+        slot = me - (me - peer + DEVICES - 1) // DEVICES
+        pltpu.make_async_remote_copy(
+            src_ref=src, dst_ref=dst.at[slot], send_sem=sems.at[0], recv_sem=sems.at[1],
+            device_id=(peer,), device_id_type=MESH).start()
+
+    def all_of(buf, sems):
+        return pltpu.make_async_remote_copy(
+            src_ref=buf, dst_ref=buf, send_sem=sems.at[0], recv_sem=sems.at[1],
+            device_id=(peers[0],), device_id_type=MESH)
+
+    for peer in peers[:2]:
+        send(st_ref, st_recv, st_sem, peer)
+    for peer in peers[:2]:
+        send(q_ref, q_recv, q_sem, peer)
+    for peer in peers[2:]:
+        send(st_ref, st_recv, st_sem, peer)
+    for peer in peers[2:]:
+        send(q_ref, q_recv, q_sem, peer)
+    all_of(st_recv, st_sem).wait_recv()
     parts = [mine] + [st_recv[k] for k in range(len(peers))]
     top = functools.reduce(jnp.maximum, parts)
     norm = top + jnp.log(functools.reduce(jnp.add, [jnp.exp(p - top) for p in parts]))
     norm = jnp.sum(jnp.where(diagonal, norm, 0.0), axis=1, keepdims=True)
     norm_ref[...] = jnp.broadcast_to(norm, norm_ref.shape)
-    for copy in q_copies:
-        copy.wait()
+    all_of(q_recv, q_sem).wait_recv()
     candz_ref[...] = functools.reduce(jnp.add, [q_recv[k] for k in range(len(peers))], q_ref[...])
+    all_of(st_recv, st_sem).wait_send()
+    all_of(q_recv, q_sem).wait_send()
 
 
 def finish_kernel(z_ref, norm_ref, candz_ref, lp_hbm, q_hbm, buf, q_ref, sem):
@@ -182,10 +190,10 @@
                 pltpu.VMEM((batch, LANES), f32),
                 pltpu.VMEM((batch, LANES), f32),
                 pltpu.VMEM((batch, LANES), f32),
-                pltpu.VMEM((len(OFFSETS), batch, LANES), f32),
+                pltpu.VMEM((DEVICES - 1, batch, LANES), f32),
                 pltpu.VMEM((1, LANES), f32),
-                pltpu.VMEM((len(OFFSETS), 1, LANES), f32),
-                dma((SLOTS,)), dma((4,)), dma((2, 7)), dma((2, 7)),
+                pltpu.VMEM((DEVICES - 1, 1, LANES), f32),
+                dma((SLOTS,)), dma((4,)), dma((2,)), dma((2,)),
             ],
             compiler_params=pltpu.CompilerParams(
                 collective_id=0, has_side_effects=True, vmem_limit_bytes=48 * 1024 * 1024),

time: 50.3 us -> 49.5 us (0.984)
  Pallas kernels: 48.9 us -> 48.1 us
    pallas_call x1, Pallas kernels: 46.8 us -> 46.1 us  [per_device(): pl.pallas_call(functools.partial(stream_kernel, axis, rows), out_shape=(p...]
where the time goes in v4:
time: 49.5 us; the launch traced here: 49.4 us
  Pallas kernels  48.1 us (97%)
  between operations  1.29 us (3%)
    pallas_call x1, Pallas kernels, per_device(): pl.pallas_call(functools.partial(stream_kernel, axis, rows), out_shape=(p...  46.1 us
    pallas_call x1, Pallas kernels, per_device(): pl.pallas_call(finish_kernel, out_shape=(jax.ShapeDtypeStruct((batch, row...  2.03 us

profile of v4, /device:TPU:0, one launch (start us, length us, event | category | flops | bytes accessed | tf_op | source)
XLA Modules:
  0.0 49.4 jit_solution(5479781736821200316)
XLA Ops:
  1.3 46.1 %shard_map.77 = (f32[32,31360]{1,0:T(8,128)S(1)}, f32[32,128]{1,0:T(8,128)S(1)}, f32[32,128]{1,0:T(8,128)S(1)}) custom-call(f32[1]{0:T(128)} %bitcast.3.t_ref, bf16[32,2048]{1,0:T(8,128)(2,1)} %x_hbm.1, bf16[16,128]{1,0:T(8,128)(2,1)} %bitcast.4, bf16[16,128]{1,0:T(8,128)(2,1)} %bitcast.5, s32[32,128]{1,0:T(8,128)} %cand_hbm.1, bf16[31360,2048]{1,0:T(8,128)(2,1)} %emb_hbm.1), custom_call_target="tpu_custom_call" | custom-call | tf_op jit(solution)/shard_map/pallas_call | solution.py:176
  47.4 2.0 %shard_map.78 = (f32[32,31360]{1,0:T(8,128)}, f32[32,128]{1,0:T(8,128)}) custom-call(f32[32,31360]{1,0:T(8,128)S(1)} %get-tuple-element.5.z_ref, f32[32,128]{1,0:T(8,128)S(1)} %get-tuple-element.6.norm_ref, f32[32,128]{1,0:T(8,128)S(1)} %get-tuple-element.7.candz_ref), custom_call_target="tpu_custom_call" | custom-call | tf_op jit(solution)/shard_map/pallas_call | solution.py:201

commit v5 on v4

--- a/solution.py
+++ b/solution.py
@@ -20,13 +20,13 @@
     return [k + (k + DEVICES - me) // DEVICES for k in range(DEVICES - 1)]
 
 
-def stream_kernel(axis, rows, t_ref, x_hbm, w_hbm, b_hbm, cand_hbm, emb_hbm, z_ref, norm_ref, candz_ref,
-                  ebuf, et_ref, x_ref, w_ref, b_ref, cand_ref, a_ref, m_ref, s_ref, q_ref, q_recv, st_ref, st_recv,
+def stream_kernel(axis, rows, x_hbm, w_hbm, b_hbm, cand_hbm, t_hbm, emb_hbm, z_ref, norm_ref, candz_ref,
+                  ebuf, et_ref, x_ref, w_ref, b_ref, cand_ref, t_ref, a_ref, m_ref, s_ref, q_ref, q_recv, st_ref, st_recv,
                   ecopy_sem, in_sem, q_sem, st_sem):
     width = x_ref.shape[1]
     chunks = rows // CHUNK
     inputs = [pltpu.make_async_copy(src, dst, in_sem.at[n]) for n, (src, dst) in enumerate(
-        [(x_hbm, x_ref), (w_hbm, w_ref), (b_hbm, b_ref), (cand_hbm, cand_ref)])]
+        [(x_hbm, x_ref), (w_hbm, w_ref), (b_hbm, b_ref), (cand_hbm, cand_ref), (t_hbm, t_ref)])]
     for copy in inputs:
         copy.start()
 
@@ -171,13 +171,13 @@
         f32, bf16 = jnp.float32, jnp.bfloat16
         dma = pltpu.SemaphoreType.DMA
         block = (width // LANES, LANES)
-        small = [hidden, ln_weight.reshape(block), ln_bias.reshape(block), cand_ids]
-        small = [pltpu.with_memory_space_constraint(v, pltpu.HBM) for v in small]
+        small = [hidden, ln_weight.reshape(block), ln_bias.reshape(block), cand_ids, temperature.reshape(1)]
+        small = [pltpu.with_memory_space_constraint(v, pltpu.HBM) for v in small[:4]] + small[4:]
         z, norm, candz = pl.pallas_call(
             functools.partial(stream_kernel, axis, rows),
             out_shape=(pltpu.VMEM((batch, rows), f32), pltpu.VMEM((batch, LANES), f32),
                        pltpu.VMEM((batch, LANES), f32)),
-            in_specs=[pl.BlockSpec(memory_space=pltpu.SMEM)] + [hbm] * 5,
+            in_specs=[hbm] * 6,
             out_specs=(vmem, vmem, vmem),
             scratch_shapes=[
                 pltpu.VMEM((SLOTS, CHUNK, width), bf16),
@@ -186,6 +186,7 @@
                 pltpu.VMEM(block, bf16),
                 pltpu.VMEM(block, bf16),
                 pltpu.VMEM((batch, LANES), jnp.int32),
+                pltpu.SMEM((1,), f32),
                 pltpu.VMEM((batch, width), bf16),
                 pltpu.VMEM((batch, LANES), f32),
                 pltpu.VMEM((batch, LANES), f32),
@@ -193,11 +194,11 @@
                 pltpu.VMEM((DEVICES - 1, batch, LANES), f32),
                 pltpu.VMEM((1, LANES), f32),
                 pltpu.VMEM((DEVICES - 1, 1, LANES), f32),
-                dma((SLOTS,)), dma((4,)), dma((2,)), dma((2,)),
+                dma((SLOTS,)), dma((5,)), dma((2,)), dma((2,)),
             ],
             compiler_params=pltpu.CompilerParams(
                 collective_id=0, has_side_effects=True, vmem_limit_bytes=48 * 1024 * 1024),
-        )(temperature.reshape(1), *small, emb)
+        )(*small, emb)
         return pl.pallas_call(
             finish_kernel,
             out_shape=(jax.ShapeDtypeStruct((batch, rows), f32), jax.ShapeDtypeStruct((batch, LANES), f32)),

time: 49.5 us -> 48.6 us (0.982)
  Pallas kernels: 48.1 us -> 47.2 us
    pallas_call x1, Pallas kernels: 46.1 us -> 45.2 us  [per_device(): pl.pallas_call(functools.partial(stream_kernel, axis, rows), out_shape=(p...]
where the time goes in v5:
time: 48.6 us; the launch traced here: 48.5 us
  Pallas kernels  47.2 us (97%)
  between operations  1.29 us (3%)
    pallas_call x1, Pallas kernels, per_device(): pl.pallas_call(functools.partial(stream_kernel, axis, rows), out_shape=(p...  45.2 us
    pallas_call x1, Pallas kernels, per_device(): pl.pallas_call(finish_kernel, out_shape=(jax.ShapeDtypeStruct((batch, row...  2.03 us

profile of v5, /device:TPU:0, one launch (start us, length us, event | category | flops | bytes accessed | tf_op | source)
XLA Modules:
  0.0 48.5 jit_solution(8204739188363641841)
XLA Ops:
  1.3 45.2 %shard_map.77 = (f32[32,31360]{1,0:T(8,128)S(1)}, f32[32,128]{1,0:T(8,128)S(1)}, f32[32,128]{1,0:T(8,128)S(1)}) custom-call(bf16[32,2048]{1,0:T(8,128)(2,1)} %x_hbm.1, bf16[16,128]{1,0:T(8,128)(2,1)} %bitcast.4, bf16[16,128]{1,0:T(8,128)(2,1)} %bitcast.5, s32[32,128]{1,0:T(8,128)} %cand_hbm.1, f32[1]{0:T(128)} %bitcast.3.t_hbm, bf16[31360,2048]{1,0:T(8,128)(2,1)} %emb_hbm.1), custom_call_target="tpu_custom_call" | custom-call | tf_op jit(solution)/shard_map/pallas_call | solution.py:176
  46.5 2.0 %shard_map.78 = (f32[32,31360]{1,0:T(8,128)}, f32[32,128]{1,0:T(8,128)}) custom-call(f32[32,31360]{1,0:T(8,128)S(1)} %get-tuple-element.5.z_ref, f32[32,128]{1,0:T(8,128)S(1)} %get-tuple-element.6.norm_ref, f32[32,128]{1,0:T(8,128)S(1)} %get-tuple-element.7.candz_ref), custom_call_target="tpu_custom_call" | custom-call | tf_op jit(solution)/shard_map/pallas_call | solution.py:202

commit v6 on v5

--- a/solution.py
+++ b/solution.py
@@ -91,7 +91,7 @@
     fetch(0, 0).wait()
     logits(0, 0)
 
-    @pl.loop(1, chunks)
+    @pl.loop(1, chunks - 1)
     def _(i):
         @pl.when(i + SLOTS - 1 < chunks)
         def _():
@@ -102,16 +102,19 @@
         candidates(i - 1)
         logits(i, lax.rem(i, SLOTS))
 
+    statistics(chunks - 2)
+    candidates(chunks - 2)
+    pl.semaphore_wait(barrier, len(peers))
+    fetch(chunks - 1, (chunks - 1) % SLOTS).wait()
+    logits(chunks - 1, (chunks - 1) % SLOTS)
+    statistics(chunks - 1)
     candidates(chunks - 1)
-    statistics(chunks - 1)
     m = m_ref[...]
     row_max = jnp.max(m, axis=1, keepdims=True)
     local = row_max + jnp.log(jnp.sum(s_ref[...] * jnp.exp(m - row_max), axis=1, keepdims=True))
     diagonal = lax.broadcasted_iota(jnp.int32, m.shape, 0) == lax.broadcasted_iota(jnp.int32, m.shape, 1)
     mine = jnp.sum(jnp.where(diagonal, local, 0.0), axis=0, keepdims=True)
     st_ref[...] = mine
-
-    pl.semaphore_wait(barrier, len(peers))
 
     def send(src, dst, sems, peer):
         slot = me - (me - peer + DEVICES - 1) // DEVICES

time: 48.6 us -> 48.6 us (level)
  no operation moved by 1% of the time
where the time goes in v6:
time: 48.6 us; the launch traced here: 48.5 us
  Pallas kernels  47.2 us (97%)
  between operations  1.29 us (3%)
    pallas_call x1, Pallas kernels, per_device(): pl.pallas_call(functools.partial(stream_kernel, axis, rows), out_shape=(p...  45.2 us
    pallas_call x1, Pallas kernels, per_device(): pl.pallas_call(finish_kernel, out_shape=(jax.ShapeDtypeStruct((batch, row...  2.03 us

profile of v6, /device:TPU:0, one launch (start us, length us, event | category | flops | bytes accessed | tf_op | source)
XLA Modules:
  0.0 48.5 jit_solution(17146279084528652638)
XLA Ops:
  1.3 45.2 %shard_map.77 = (f32[32,31360]{1,0:T(8,128)S(1)}, f32[32,128]{1,0:T(8,128)S(1)}, f32[32,128]{1,0:T(8,128)S(1)}) custom-call(bf16[32,2048]{1,0:T(8,128)(2,1)} %x_hbm.1, bf16[16,128]{1,0:T(8,128)(2,1)} %bitcast.4, bf16[16,128]{1,0:T(8,128)(2,1)} %bitcast.5, s32[32,128]{1,0:T(8,128)} %cand_hbm.1, f32[1]{0:T(128)} %bitcast.3.t_hbm, bf16[31360,2048]{1,0:T(8,128)(2,1)} %emb_hbm.1), custom_call_target="tpu_custom_call" | custom-call | tf_op jit(solution)/shard_map/pallas_call | solution.py:179
  46.5 2.0 %shard_map.78 = (f32[32,31360]{1,0:T(8,128)}, f32[32,128]{1,0:T(8,128)}) custom-call(f32[32,31360]{1,0:T(8,128)S(1)} %get-tuple-element.5.z_ref, f32[32,128]{1,0:T(8,128)S(1)} %get-tuple-element.6.norm_ref, f32[32,128]{1,0:T(8,128)S(1)} %get-tuple-element.7.candz_ref), custom_call_target="tpu_custom_call" | custom-call | tf_op jit(solution)/shard_map/pallas_call | solution.py:205

commit v7 on v5

--- a/solution.py
+++ b/solution.py
@@ -9,8 +9,11 @@
 
 LANES = 128
 CHUNK = 896
-SLOTS = 5
+GROUP = 2
+SINGLES = 5
+SLOTS = 4
 DOTS = ((0, 128, False), (128, 256, False), (384, 256, True), (640, 256, True))
+GROUP_DOTS = tuple((256 * n, 256, n >= 3) for n in range(7))
 PIECES = (896, 1792, 3584, 6272, 6272, 6272, 6272)
 DEVICES = 8
 MESH = pl.DeviceIdType.MESH
@@ -30,11 +33,27 @@
     for copy in inputs:
         copy.start()
 
-    def fetch(i, slot):
-        return pltpu.make_async_copy(emb_hbm.at[pl.ds(i * CHUNK, CHUNK), :], ebuf.at[slot], ecopy_sem.at[slot])
-
-    for i in range(SLOTS):
-        fetch(i, i).start()
+    groups = (chunks - SINGLES) // GROUP
+    transfers = groups + SINGLES
+
+    def fetch(n, single):
+        first = (groups * GROUP + n - groups) * CHUNK if single else n * GROUP * CHUNK
+        size = CHUNK if single else GROUP * CHUNK
+        slot = lax.rem(n, SLOTS)
+        return pltpu.make_async_copy(
+            emb_hbm.at[pl.ds(first, size), :], ebuf.at[slot, pl.ds(0, size), :], ecopy_sem.at[slot])
+
+    def begin(n):
+        @pl.when(n < groups)
+        def _():
+            fetch(n, False).start()
+
+        @pl.when((n >= groups) & (n < transfers))
+        def _():
+            fetch(n, True).start()
+
+    for n in range(SLOTS):
+        fetch(n, False).start()
 
     me = lax.axis_index(axis)
     peers = peers_of(me)
@@ -57,12 +76,12 @@
     q_ref[...] = jnp.zeros(q_ref.shape, jnp.float32)
     temp = t_ref[0]
 
-    def logits(i, slot):
-        for n, (first, size, flip) in enumerate(DOTS):
+    def logits(i, slot, dots):
+        for n, (first, size, flip) in enumerate(dots):
             tile = ebuf[slot, first:first + size, :]
             if flip:
-                et_ref[n, :, :size] = tile.T
-                z = jnp.dot(a_ref[...], et_ref[n, :, :size], preferred_element_type=jnp.float32)
+                et_ref[n] = tile.T
+                z = jnp.dot(a_ref[...], et_ref[n], preferred_element_type=jnp.float32)
             else:
                 z = lax.dot_general(tile, a_ref[...], (((1,), (1,)), ((), ())), preferred_element_type=jnp.float32).T
             z_ref[:, pl.ds(pl.multiple_of(i * CHUNK + first, LANES), size)] = z / temp
@@ -88,20 +107,33 @@
         m_ref[...] = new
         s_ref[...] = total
 
-    fetch(0, 0).wait()
-    logits(0, 0)
-
-    @pl.loop(1, chunks)
-    def _(i):
-        @pl.when(i + SLOTS - 1 < chunks)
-        def _():
-            fetch(i + SLOTS - 1, lax.rem(i + SLOTS - 1, SLOTS)).start()
-
-        fetch(i, lax.rem(i, SLOTS)).wait()
-        statistics(i - 1)
-        candidates(i - 1)
-        logits(i, lax.rem(i, SLOTS))
-
+    def fold(i):
+        statistics(i)
+        candidates(i)
+
+    fetch(0, False).wait()
+    logits(0, 0, GROUP_DOTS)
+
+    @pl.loop(1, groups)
+    def _(n):
+        begin(n + SLOTS - 1)
+        fetch(n, False).wait()
+        for j in range(GROUP):
+            fold((n - 1) * GROUP + j)
+        logits(n * GROUP, lax.rem(n, SLOTS), GROUP_DOTS)
+
+    for j in range(GROUP - 1):
+        fold((groups - 1) * GROUP + j)
+
+    @pl.loop(groups, transfers)
+    def _(n):
+        begin(n + SLOTS - 1)
+        fetch(n, True).wait()
+        i = groups * GROUP + n - groups
+        fold(i - 1)
+        logits(i, lax.rem(n, SLOTS), DOTS)
+
+    pl.semaphore_wait(barrier, len(peers))
     candidates(chunks - 1)
     statistics(chunks - 1)
     m = m_ref[...]
@@ -110,8 +142,6 @@
     diagonal = lax.broadcasted_iota(jnp.int32, m.shape, 0) == lax.broadcasted_iota(jnp.int32, m.shape, 1)
     mine = jnp.sum(jnp.where(diagonal, local, 0.0), axis=0, keepdims=True)
     st_ref[...] = mine
-
-    pl.semaphore_wait(barrier, len(peers))
 
     def send(src, dst, sems, peer):
         slot = me - (me - peer + DEVICES - 1) // DEVICES
@@ -180,8 +210,8 @@
             in_specs=[hbm] * 6,
             out_specs=(vmem, vmem, vmem),
             scratch_shapes=[
-                pltpu.VMEM((SLOTS, CHUNK, width), bf16),
-                pltpu.VMEM((len(DOTS), width, 256), bf16),
+                pltpu.VMEM((SLOTS, GROUP * CHUNK, width), bf16),
+                pltpu.VMEM((len(GROUP_DOTS), width, 256), bf16),
                 pltpu.VMEM((batch, width), bf16),
                 pltpu.VMEM(block, bf16),
                 pltpu.VMEM(block, bf16),
@@ -197,7 +227,7 @@
                 dma((SLOTS,)), dma((5,)), dma((2,)), dma((2,)),
             ],
             compiler_params=pltpu.CompilerParams(
-                collective_id=0, has_side_effects=True, vmem_limit_bytes=48 * 1024 * 1024),
+                collective_id=0, has_side_effects=True, vmem_limit_bytes=52 * 1024 * 1024),
         )(*small, emb)
         return pl.pallas_call(
             finish_kernel,

time: 48.6 us -> 48.6 us (level)
  no operation moved by 1% of the time
where the time goes in v7:
time: 48.6 us; the launch traced here: 48.5 us
  Pallas kernels  47.2 us (97%)
  between operations  1.29 us (3%)
    pallas_call x1, Pallas kernels, per_device(): pl.pallas_call(functools.partial(stream_kernel, axis, rows), out_shape=(p...  45.1 us
    pallas_call x1, Pallas kernels, per_device(): pl.pallas_call(finish_kernel, out_shape=(jax.ShapeDtypeStruct((batch, row...  2.03 us

profile of v7, /device:TPU:0, one launch (start us, length us, event | category | flops | bytes accessed | tf_op | source)
XLA Modules:
  0.0 48.5 jit_solution(10262916290191074043)
XLA Ops:
  1.3 45.1 %shard_map.77 = (f32[32,31360]{1,0:T(8,128)S(1)}, f32[32,128]{1,0:T(8,128)S(1)}, f32[32,128]{1,0:T(8,128)S(1)}) custom-call(bf16[32,2048]{1,0:T(8,128)(2,1)} %x_hbm.1, bf16[16,128]{1,0:T(8,128)(2,1)} %bitcast.4, bf16[16,128]{1,0:T(8,128)(2,1)} %bitcast.5, s32[32,128]{1,0:T(8,128)} %cand_hbm.1, f32[1]{0:T(128)} %bitcast.3.t_hbm, bf16[31360,2048]{1,0:T(8,128)(2,1)} %emb_hbm.1), custom_call_target="tpu_custom_call" | custom-call | tf_op jit(solution)/shard_map/pallas_call | solution.py:206
  46.4 2.0 %shard_map.78 = (f32[32,31360]{1,0:T(8,128)}, f32[32,128]{1,0:T(8,128)}) custom-call(f32[32,31360]{1,0:T(8,128)S(1)} %get-tuple-element.5.z_ref, f32[32,128]{1,0:T(8,128)S(1)} %get-tuple-element.6.norm_ref, f32[32,128]{1,0:T(8,128)S(1)} %get-tuple-element.7.candz_ref), custom_call_target="tpu_custom_call" | custom-call | tf_op jit(solution)/shard_map/pallas_call | solution.py:232
